TPU v7x, 32 devices: a whole 2x2x4 slice. The times are simulated.
32 devices in a mesh: section: 4 (over y, x), dp: 8 (over z, core).
Axes of the slice: x: 2, y: 2, z: 4, core: 2. Of those that a mesh axis runs over, the one named last changes fastest.
Arguments:
- activations: bfloat16 [4, 8, 257, 1792], P('section', 'dp'), may hold values from -6 to 6
- saved: bfloat16 [4, 8, 257, 1792], P('section', 'dp'), may hold values from -6 to 6
- cotangents: bfloat16 [4, 8, 257, 1792], P('section', 'dp'), may hold values from -1.1953125 to 1.1953125
- projection: bfloat16 [4, 1792, 1792], P('section'), may hold values from -0.125 to 0.125
- section_gain: float32 [4, 1792], P('section'), may hold values from 0.5 to 1.5
- final_gain: float32 [1792], replicated, may hold values from 0.5 to 1.5
- head_weight: bfloat16 [1792, 1024], P('section'), may hold values from -0.125 to 0.125
- text_embed: bfloat16 [8, 1024], P('dp'), may hold values from -6 to 6
- labels: int32 [8], P('dp'), may hold values from 0 to 7, each once
Outputs:
- next_act: bfloat16 [4, 8, 257, 1792], P('section', 'dp')
- next_grad: bfloat16 [4, 8, 257, 1792], P('section', 'dp')
- mean_loss: float32 [4], P('section')
Inputs may be any that keep to these rules, and one draw needn't show every extreme that they name: labels holds each caption index once.
All inputs are finite; a program needn't handle non-finite values.
Results may differ from a plain program's by a relative error of at most 0.0039.
Values may be sent and summed in bfloat16 or wider, within the bound.
A program may use at most 64 MiB of HBM per device.

v0:
```python
import jax
import jax.numpy as jnp
from jax import lax
from jax.sharding import PartitionSpec as P

epsilon = 1e-06
logit_scale = 100.0


def shifted(value, axis, steps):
    count = lax.axis_size(axis)
    first, last = (max(0, -steps), min(count, count - steps))
    return lax.ppermute(value, axis, [(source, source + steps) for source in range(first, last)])


def spread(block, axis, owner):
    block = jnp.where(lax.axis_index(axis) == owner, block, jnp.zeros_like(block))
    return lax.psum(block, axis)


def norm_rows(values):
    centre = jnp.mean(values, axis=-1, keepdims=True)
    centred = values - centre
    variance = jnp.mean(centred * centred, axis=-1, keepdims=True)
    inverse = lax.rsqrt(variance + epsilon)
    return (centred * inverse, inverse)


def unit_rows(values):
    inverse = lax.rsqrt(jnp.sum(values * values, axis=-1, keepdims=True) + epsilon)
    return (values * inverse, inverse)


def forward_block(block_in, weight, scale_row):
    block_shape = block_in.shape
    standard, inverse = norm_rows(block_in.astype(jnp.float32))
    normed = (standard * scale_row).astype(jnp.bfloat16)
    mixed = jnp.dot(normed.reshape(-1, block_shape[-1]), weight, preferred_element_type=jnp.float32)
    return (block_in.astype(jnp.float32) + mixed.reshape(block_shape)).astype(jnp.bfloat16)


def backward_block(cotangent, restored, weight, scale_row):
    block_shape = restored.shape
    standard, inverse = norm_rows(restored.astype(jnp.float32))
    d_normed = lax.dot_general(
        cotangent.reshape(-1, block_shape[-1]),
        weight,
        (((1,), (1,)), ((), ())),
        preferred_element_type=jnp.float32,
    ).reshape(block_shape)
    d_standard = d_normed * scale_row
    d_input = cotangent.astype(jnp.float32) + inverse * (
        d_standard
        - jnp.mean(d_standard, axis=-1, keepdims=True)
        - standard * jnp.mean(d_standard * standard, axis=-1, keepdims=True)
    )
    return d_input.astype(jnp.bfloat16)


def contrastive(logits, label_values):
    count = logits.shape[0]
    targets = (label_values[:, None] == jnp.arange(count).astype(jnp.float32)[None, :]).astype(
        jnp.float32
    )
    row_lse = jax.nn.logsumexp(logits, axis=1)
    col_lse = jax.nn.logsumexp(logits, axis=0)
    picked = jnp.sum(logits * targets, axis=1)
    col_picked = jnp.sum(col_lse[None, :] * targets, axis=1)
    loss_value = 0.5 * jnp.mean(row_lse - picked) + 0.5 * jnp.mean(col_picked - picked)
    row_prob = jnp.exp(logits - row_lse[:, None])
    col_prob = jnp.exp(logits - col_lse[None, :])
    d_logits = 0.5 * (row_prob - targets + (col_prob - targets))
    return (loss_value, d_logits)


def local(
    activations,
    saved,
    cotangents,
    projection,
    section_gain,
    final_gain,
    head_weight,
    text_embed,
    labels,
):
    sections = lax.axis_size("section")
    section_index = lax.axis_index("section")
    is_last = section_index == sections - 1
    weight = projection[0]
    scale_row = section_gain[0]
    incoming = activations[0]
    block_out = forward_block(incoming, weight, scale_row)
    next_act = shifted(block_out[None], "section", 1)
    d_input = backward_block(cotangents[0], saved[0], weight, scale_row)
    passed_grad = shifted(d_input[None], "section", -1)
    pooled = jnp.mean(block_out.astype(jnp.float32), axis=1)
    pooled_std, pooled_inv = norm_rows(pooled)
    pooled_norm = (pooled_std * final_gain).astype(jnp.bfloat16)
    shared = spread(pooled_norm, "section", sections - 1)
    row_count = head_weight.shape[0]
    my_columns = lax.dynamic_slice_in_dim(shared, section_index * row_count, row_count, 1)
    embedding = lax.psum(
        jnp.dot(my_columns, head_weight, preferred_element_type=jnp.float32), "section"
    )
    image_unit, image_inv = unit_rows(embedding)
    own_count = image_unit.shape[0]
    text_unit, text_inv = unit_rows(text_embed.astype(jnp.float32))
    all_image, all_text, all_labels = (
        lax.all_gather(image_unit, "dp", axis=0, tiled=True),
        lax.all_gather(text_unit, "dp", axis=0, tiled=True),
        lax.all_gather(labels.astype(jnp.float32), "dp", axis=0, tiled=True),
    )
    logits = logit_scale * jnp.dot(all_image, all_text.T, precision=lax.Precision.HIGHEST)
    loss_value, d_logits = contrastive(logits, all_labels)
    own_rows = lax.dynamic_slice_in_dim(d_logits, lax.axis_index("dp") * own_count, own_count, 0)
    d_image = logit_scale * jnp.dot(own_rows, all_text, precision=lax.Precision.HIGHEST)
    d_embedding = (
        (d_image - image_unit * jnp.sum(d_image * image_unit, axis=-1, keepdims=True)) * image_inv
    ).astype(jnp.bfloat16)
    partial_value = lax.dot_general(
        d_embedding, head_weight, (((1,), (1,)), ((), ())), preferred_element_type=jnp.float32
    )
    d_pooled_norm = lax.all_gather(partial_value, "section", axis=1, tiled=True)
    d_std = d_pooled_norm * final_gain
    d_pooled = pooled_inv * (
        d_std
        - jnp.mean(d_std, axis=-1, keepdims=True)
        - pooled_std * jnp.mean(d_std * pooled_std, axis=-1, keepdims=True)
    )
    token_count = block_out.shape[1]
    loss_grad = jnp.broadcast_to((d_pooled / token_count)[:, None, :], block_out.shape).astype(
        jnp.bfloat16
    )
    next_grad = jnp.where(is_last, loss_grad[None], passed_grad)
    mean_loss = jnp.where(is_last, loss_value, jnp.float32(0.0))[None]
    return (next_act, next_grad, mean_loss)


def solution(mesh):
    return jax.shard_map(
        local,
        mesh=mesh,
        in_specs=(
            P("section", "dp", None, None),
            P("section", "dp", None, None),
            P("section", "dp", None, None),
            P("section", None, None),
            P("section", None),
            P(),
            P("section", None),
            P("dp", None),
            P("dp"),
        ),
        out_specs=(P("section", "dp", None, None), P("section", "dp", None, None), P("section")),
        check_vma=False,
    )
```

profile of v0, /device:TPU:0, one launch (start us, length us, event | category | flops | bytes accessed | tf_op | source)
XLA Modules:
  0.0 115.6 jit_solution(8883535703884968360)
XLA Ops:
  0.7 1.5 %convert_reduce_fusion = f32[257]{0:T(512)S(1)} fusion(bf16[1,1,257,1792]{3,2,1,0:T(8,128)(2,1)} %param.9), kind=kLoop, calls=%fused_computation.6 | loop fusion | flops 920831 | bytes 922116 | tf_op jit(solution)/shard_map/reduce_sum | solution.py:22
  2.2 1.6 %fusion.30 = f32[257]{0:T(512)S(1)} fusion(bf16[1,1,257,1792]{3,2,1,0:T(8,128)(2,1)} %param.9, f32[257]{0:T(512)S(1)} %broadcast_multiply_fusion.5), kind=kLoop, calls=%fused_computation.31 | loop fusion | flops 1841919 | bytes 923144 | tf_op jit(solution)/shard_map/reduce_sum | solution.py:24
  3.9 5.8 %convert_reduce_fusion.2 = (f32[1792]{0:T(1024)S(1)}, bf16[257,1792]{1,0:T(8,128)(2,1)}) fusion(bf16[1,1792,1792]{2,1,0:T(8,128)(2,1)} %param.12, bf16[1,1,257,1792]{3,2,1,0:T(8,128)(2,1)S(1)} %copy-done.2, f32[1792]{0:T(1024)S(1)} %reduce.23, f32[257]{0:T(512)S(1)} %add_rsqrt_fusion.1, f32[257]{0:T(512)S(1)} %broadcast_multiply_fusion.5), kind=kOutput, calls=%fused_computation.32 | convolution fusion | flops 1655193344 | bytes 8281096 | tf_op jit(solution)/shard_map/dot_general | solution.py:38
  9.7 5.0 %collective-permute-start = (bf16[1,1,257,1792]{3,2,1,0:T(8,128)(2,1)}, bf16[1,1,257,1792]{3,2,1,0:T(8,128)(2,1)S(1)}, u32[]{:S(2)}, u32[]{:S(2)}) collective-permute-start(bf16[1,1,257,1792]{3,2,1,0:T(8,128)(2,1)} %bitcast.4), channel_id=1, source_target_pairs={{0,8},{8,16},{16,24},{1,9},{9,17},{17,25},{2,10},{10,18},{18,26},{... | collective-permute-start | bytes 2763272 | tf_op jit(solution)/shard_map/ppermute | solution.py:13
  14.8 0.2 convert_reduce_fusion.1
  15.0 0.4 fusion.15
  15.4 4.9 %fusion.68 = (f32[257]{0:T(512)S(1)}, f32[257]{0:T(512)S(1)}, f32[257,1792]{1,0:T(8,128)S(1)}) fusion(f32[257]{0:T(512)S(1)} %add_rsqrt_fusion, f32[257]{0:T(512)S(1)} %broadcast_multiply_fusion.4, bf16[1,1,257,1792]{3,2,1,0:T(8,128)(2,1)S(1)} %copy-done.1, f32[1792]{0:T(1024)S(1)} %reduce.23, bf16[1,1792,1792]{2,1,0:T(8,128)(2,1)} %param.12, ...), kind=kOutput, calls=%fused_computation.102 | convolution fusion | flops 1653812992 | bytes 10118160 | tf_op jit(solution)/shard_map/dot_general | solution.py:45
  20.4 0.8 fusion.33
  21.2 1.3 %collective-permute-start.1 = (bf16[1,1,257,1792]{3,2,1,0:T(8,128)(2,1)S(1)}, bf16[1,1,257,1792]{3,2,1,0:T(8,128)(2,1)}, u32[]{:S(2)}, u32[]{:S(2)}) collective-permute-start(bf16[1,1,257,1792]{3,2,1,0:T(8,128)(2,1)S(1)} %fusion.33), channel_id=1, source_target_pairs={{8,0},{16,8},{24,16},{9,1},{17,9},{25,17},{10,2},{18,10},{26,18},{... | collective-permute-start | bytes 2763272 | tf_op jit(solution)/shard_map/ppermute | solution.py:13
  23.2 0.6 multiply_reduce_fusion.4
  24.5 0.6 dynamic-slice
  25.1 0.7 convert_dynamic-update-slice_fusion
  25.8 16.4 %all-reduce = f32[8]{0:T(128)S(1)} all-reduce(f32[8]{0:T(128)S(1)} %convert_dynamic-update-slice_fusion), channel_id=1, replica_groups=mesh['section'=4,'dp'=8] {'dp'}, use_global_device_ids=true, to_apply=%add | all-reduce | flops 8 | bytes 64
  42.2 14.1 %all-gather.2 = f32[8,1,1024]{2,1,0:T(1,128)S(1)} all-gather(f32[1,1,1024]{2,1,0:T(1,128)S(1)} %multiply_bitcast_fusion), channel_id=1, replica_groups=mesh['section'=4,'dp'=8] {'dp'}, dimensions={0}, use_global_device_ids=true | all-gather | bytes 36864 | tf_op jit(solution)/shard_map/all_gather | solution.py:111
  56.3 0.6 multiply_reduce_fusion.2
  57.5 0.6 multiply_reduce_fusion.1
  58.9 11.8 %psum.14 = bf16[1,1792]{1,0:T(2,128)(2,1)S(1)} all-reduce(bf16[1,1792]{1,0:T(2,128)(2,1)S(1)} %select_n.52), channel_id=1, replica_groups=mesh['section'=4,'dp'=8] {'section'}, use_global_device_ids=true, to_apply=%region_5.0 | all-reduce | flops 1792 | bytes 7168 | tf_op jit(solution)/shard_map/psum | solution.py:18
  70.7 0.3 fusion.58
  70.9 7.9 %psum.15 = f32[1,1024]{1,0:T(1,128)S(1)} all-reduce(f32[1,1024]{1,0:T(1,128)S(1)} %fusion.58), channel_id=1, replica_groups=mesh['section'=4,'dp'=8] {'section'}, use_global_device_ids=true, to_apply=%region_6.0 | all-reduce | flops 1024 | bytes 8192 | tf_op jit(solution)/shard_map/psum | solution.py:103
  78.8 0.6 multiply_reduce_fusion.5
  80.1 14.1 %all-gather.1 = f32[8,1,1024]{2,1,0:T(1,128)S(1)} all-gather(f32[1,1,1024]{2,1,0:T(1,128)S(1)} %fusion.67), channel_id=1, replica_groups=mesh['section'=4,'dp'=8] {'dp'}, dimensions={0}, use_global_device_ids=true | all-gather | bytes 36864 | tf_op jit(solution)/shard_map/all_gather | solution.py:110
  94.2 0.3 fusion.70
  94.5 0.2 fusion.49
  94.9 0.6 subtract_reduce_fusion
  95.8 0.6 dynamic-slice.1
  98.4 0.6 multiply_reduce_fusion.3
  99.0 1.0 fusion.52
  100.0 0.2 dynamic-update-slice.1
  100.2 9.2 %all-reduce.1 = f32[1792]{0:T(1024)S(1)} all-reduce(f32[1792]{0:T(1024)S(1)} %dynamic-update-slice.1), channel_id=2, replica_groups=mesh['section'=4,'dp'=8] {'section'}, use_global_device_ids=true, to_apply=%add.1 | all-reduce | flops 1792 | bytes 14336
  109.4 0.7 fusion.69
  111.4 2.2 %broadcast_select_fusion = bf16[1,1,257,1792]{3,2,1,0:T(8,128)(2,1)} fusion(bf16[1,1,257,1792]{3,2,1,0:T(8,128)(2,1)} %collective-permute-done.1, pred[]{:T(512)S(6)} %eq.8, bf16[1792]{0:T(1024)(128)(2,1)S(1)} %multiply_convert_fusion), kind=kLoop, calls=%fused_computation.40 | loop fusion | flops 460544 | bytes 1845761 | tf_op jit(solution)/shard_map/jit(_where)/select_n | solution.py:135
  113.6 0.9 copy.34
  (40 shorter events, 0.6 us)
Async XLA Ops:
  0.6 70.0 %copy-start = (bf16[448,1024]{1,0:T(8,128)(2,1)S(1)}, bf16[448,1024]{1,0:T(8,128)(2,1)}, u32[]{:S(2)}) copy-start(bf16[448,1024]{1,0:T(8,128)(2,1)} %param.15) | copy-start | bytes 2752516
  0.6 3.2 %copy-start.2 = (bf16[1,1,257,1792]{3,2,1,0:T(8,128)(2,1)S(1)}, bf16[1,1,257,1792]{3,2,1,0:T(8,128)(2,1)}, u32[]{:S(2)}) copy-start(bf16[1,1,257,1792]{3,2,1,0:T(8,128)(2,1)} %param.9) | copy-start | bytes 2763268
  0.7 3.2 %copy-start.6 = (f32[1,1792]{1,0:T(1,128)S(1)}, f32[1,1792]{1,0:T(1,128)}, u32[]{:S(2)}) copy-start(f32[1,1792]{1,0:T(1,128)} %param.13) | copy-start | bytes 21508
  3.9 10.9 %copy-start.1 = (bf16[1,1,257,1792]{3,2,1,0:T(8,128)(2,1)S(1)}, bf16[1,1,257,1792]{3,2,1,0:T(8,128)(2,1)}, u32[]{:S(2)}) copy-start(bf16[1,1,257,1792]{3,2,1,0:T(8,128)(2,1)} %param.10) | copy-start | bytes 2763268
  9.7 5.7 %copy-start.3 = (bf16[1,1,257,1792]{3,2,1,0:T(8,128)(2,1)S(1)}, bf16[1,1,257,1792]{3,2,1,0:T(8,128)(2,1)}, u32[]{:S(2)}) copy-start(bf16[1,1,257,1792]{3,2,1,0:T(8,128)(2,1)} %param.11) | copy-start | bytes 2763268
  9.7 101.7 %collective-permute-start = (bf16[1,1,257,1792]{3,2,1,0:T(8,128)(2,1)}, bf16[1,1,257,1792]{3,2,1,0:T(8,128)(2,1)S(1)}, u32[]{:S(2)}, u32[]{:S(2)}) collective-permute-start(bf16[1,1,257,1792]{3,2,1,0:T(8,128)(2,1)} %bitcast.4), channel_id=1, source_target_pairs={{0,8},{8,16},{16,24},{1,9},{9,17},{17,25},{2,10},{10,18},{18,26},{... | collective-permute-start | bytes 2763272 | tf_op jit(solution)/shard_map/ppermute | solution.py:13
  20.4 2.8 %copy-start.5 = (bf16[1,1024]{1,0:T(2,128)(2,1)S(1)}, bf16[1,1024]{1,0:T(2,128)(2,1)}, u32[]{:S(2)}) copy-start(bf16[1,1024]{1,0:T(2,128)(2,1)} %param.16) | copy-start | bytes 6148
  20.4 4.0 %copy-start.8 = (u32[32]{0:T(128)S(1)}, u32[32]{0:T(128)}, u32[]{:S(2)}) copy-start(u32[32]{0:T(128)} %constant.76) | copy-start | bytes 388
  20.4 38.4 %copy-start.4 = (f32[1792]{0:T(1024)S(1)}, f32[1792]{0:T(1024)}, u32[]{:S(2)}) copy-start(f32[1792]{0:T(1024)} %param.14) | copy-start | bytes 21508
  20.4 75.4 %copy-start.7 = (u32[32]{0:T(128)S(1)}, u32[32]{0:T(128)}, u32[]{:S(2)}) copy-start(u32[32]{0:T(128)} %constant.81) | copy-start | bytes 388
  21.2 90.2 %collective-permute-start.1 = (bf16[1,1,257,1792]{3,2,1,0:T(8,128)(2,1)S(1)}, bf16[1,1,257,1792]{3,2,1,0:T(8,128)(2,1)}, u32[]{:S(2)}, u32[]{:S(2)}) collective-permute-start(bf16[1,1,257,1792]{3,2,1,0:T(8,128)(2,1)S(1)} %fusion.33), channel_id=1, source_target_pairs={{8,0},{16,8},{24,16},{9,1},{17,9},{25,17},{10,2},{18,10},{26,18},{... | collective-permute-start | bytes 2763272 | tf_op jit(solution)/shard_map/ppermute | solution.py:13
where the time goes:
time: 116 us
  blocking collectives  73.4 us (63%)
  matrix products  12.5 us (11%)
  other arithmetic  12.4 us (11%)
  between operations  8.64 us (7%)
  starting transfers between devices  6.34 us (5%)
  local copies, waits for them, and re-layouts  2.44 us (2%)
    unnamed x2, blocking collectives  25.5 us
    all_gather x1, blocking collectives, local(): lax.all_gather(image_unit, 'dp', axis=0, tiled=True)  14.1 us
    all_gather x1, blocking collectives, local(): lax.all_gather(text_unit, 'dp', axis=0, tiled=True)  14.1 us
    psum x1, blocking collectives, spread(): return lax.psum(block, axis)  11.8 us
    psum x1, blocking collectives, local(): lax.psum(jnp.dot(my_columns, head_weight, preferred_element_type=jnp.floa...  7.87 us
    ppermute x2, starting transfers between devices, shifted(): lax.ppermute(value, axis, [(source, source + steps) for source in range(f...  6.34 us
    dot_general x1, matrix products, forward_block(): jnp.dot(normed.reshape(-1, block_shape[-1]), weight, preferred_element_ty...  5.82 us
    dot_general x1, matrix products, backward_block(): lax.dot_general(cotangent.reshape(-1, block_shape[-1]), weight, (((1,), (...  4.94 us
  transfers between devices with their start and end apart: 2, of which 0 were waited for; matrix products, arithmetic and copies ran while one was open for 13% of the time, Pallas kernels for 0%

commit v1 on v0

--- a/solution.py
+++ b/solution.py
@@ -100,8 +100,11 @@
     shared = spread(pooled_norm, "section", sections - 1)
     row_count = head_weight.shape[0]
     my_columns = lax.dynamic_slice_in_dim(shared, section_index * row_count, row_count, 1)
-    embedding = lax.psum(
-        jnp.dot(my_columns, head_weight, preferred_element_type=jnp.float32), "section"
+    embedding = jnp.sum(
+        lax.all_gather(
+            jnp.dot(my_columns, head_weight, preferred_element_type=jnp.float32), "section"
+        ),
+        axis=0,
     )
     image_unit, image_inv = unit_rows(embedding)
     own_count = image_unit.shape[0]

time: 116 us -> 115 us (level)
    psum x1 -> x0, blocking collectives: 7.87 us -> none  [local(): lax.psum(jnp.dot(my_columns, head_weight, preferred_element_type=jnp.floa...]
    all_gather x0 -> x1, blocking collectives: none -> 7.23 us  [local(): lax.all_gather(jnp.dot(my_columns, head_weight, preferred_element_type=jn...]
where the time goes in v1:
time: 115 us
  blocking collectives  72.6 us (63%)
  other arithmetic  13 us (11%)
  matrix products  11.8 us (10%)
  between operations  8.64 us (8%)
  starting transfers between devices  6.34 us (6%)
  local copies, waits for them, and re-layouts  2.47 us (2%)
    unnamed x2, blocking collectives  25.4 us
    all_gather x1, blocking collectives, local(): lax.all_gather(image_unit, 'dp', axis=0, tiled=True)  14.1 us
    all_gather x1, blocking collectives, local(): lax.all_gather(text_unit, 'dp', axis=0, tiled=True)  14.1 us
    psum x1, blocking collectives, spread(): return lax.psum(block, axis)  11.8 us
    all_gather x1, blocking collectives, local(): lax.all_gather(jnp.dot(my_columns, head_weight, preferred_element_type=jn...  7.23 us
    ppermute x2, starting transfers between devices, shifted(): lax.ppermute(value, axis, [(source, source + steps) for source in range(f...  6.34 us
    dot_general x1, matrix products, forward_block(): jnp.dot(normed.reshape(-1, block_shape[-1]), weight, preferred_element_ty...  5.82 us
    dot_general x1, matrix products, backward_block(): lax.dot_general(cotangent.reshape(-1, block_shape[-1]), weight, (((1,), (...  4.94 us
  transfers between devices with their start and end apart: 2, of which 0 were waited for; matrix products, arithmetic and copies ran while one was open for 13% of the time, Pallas kernels for 0%

profile of v1, /device:TPU:0, one launch (start us, length us, event | category | flops | bytes accessed | tf_op | source)
XLA Modules:
  0.0 114.9 jit_solution(4383267107033923629)
XLA Ops:
  0.7 1.5 %convert_reduce_fusion = f32[257]{0:T(512)S(1)} fusion(bf16[1,1,257,1792]{3,2,1,0:T(8,128)(2,1)} %param.9), kind=kLoop, calls=%fused_computation.6 | loop fusion | flops 920831 | bytes 922116 | tf_op jit(solution)/shard_map/reduce_sum | solution.py:22
  2.2 1.6 %fusion.30 = f32[257]{0:T(512)S(1)} fusion(bf16[1,1,257,1792]{3,2,1,0:T(8,128)(2,1)} %param.9, f32[257]{0:T(512)S(1)} %broadcast_multiply_fusion.4), kind=kLoop, calls=%fused_computation.31 | loop fusion | flops 1841919 | bytes 923144 | tf_op jit(solution)/shard_map/reduce_sum | solution.py:24
  3.9 5.8 %convert_reduce_fusion.2 = (f32[1792]{0:T(1024)S(1)}, bf16[257,1792]{1,0:T(8,128)(2,1)}) fusion(bf16[1,1792,1792]{2,1,0:T(8,128)(2,1)} %param.12, bf16[1,1,257,1792]{3,2,1,0:T(8,128)(2,1)S(1)} %copy-done.2, f32[1792]{0:T(1024)S(1)} %reduce.27, f32[257]{0:T(512)S(1)} %add_rsqrt_fusion.1, f32[257]{0:T(512)S(1)} %broadcast_multiply_fusion.4), kind=kOutput, calls=%fused_computation.32 | convolution fusion | flops 1655193344 | bytes 8281096 | tf_op jit(solution)/shard_map/dot_general | solution.py:38
  9.7 5.0 %collective-permute-start = (bf16[1,1,257,1792]{3,2,1,0:T(8,128)(2,1)}, bf16[1,1,257,1792]{3,2,1,0:T(8,128)(2,1)S(1)}, u32[]{:S(2)}, u32[]{:S(2)}) collective-permute-start(bf16[1,1,257,1792]{3,2,1,0:T(8,128)(2,1)} %bitcast.4), channel_id=1, source_target_pairs={{0,8},{8,16},{16,24},{1,9},{9,17},{17,25},{2,10},{10,18},{18,26},{... | collective-permute-start | bytes 2763272 | tf_op jit(solution)/shard_map/ppermute | solution.py:13
  14.8 0.2 convert_reduce_fusion.1
  15.0 0.4 fusion.15
  15.4 4.9 %fusion.57 = (f32[257]{0:T(512)S(1)}, f32[257]{0:T(512)S(1)}, f32[257,1792]{1,0:T(8,128)S(1)}) fusion(f32[257]{0:T(512)S(1)} %add_rsqrt_fusion, f32[257]{0:T(512)S(1)} %broadcast_multiply_fusion.3, bf16[1,1,257,1792]{3,2,1,0:T(8,128)(2,1)S(1)} %copy-done.1, f32[1792]{0:T(1024)S(1)} %reduce.27, bf16[1,1792,1792]{2,1,0:T(8,128)(2,1)} %param.12, ...), kind=kOutput, calls=%fused_computation.91 | convolution fusion | flops 1653812992 | bytes 10118160 | tf_op jit(solution)/shard_map/dot_general | solution.py:45
  20.4 0.8 fusion.33
  21.2 1.3 %collective-permute-start.1 = (bf16[1,1,257,1792]{3,2,1,0:T(8,128)(2,1)S(1)}, bf16[1,1,257,1792]{3,2,1,0:T(8,128)(2,1)}, u32[]{:S(2)}, u32[]{:S(2)}) collective-permute-start(bf16[1,1,257,1792]{3,2,1,0:T(8,128)(2,1)S(1)} %fusion.33), channel_id=1, source_target_pairs={{8,0},{16,8},{24,16},{9,1},{17,9},{25,17},{10,2},{18,10},{26,18},{... | collective-permute-start | bytes 2763272 | tf_op jit(solution)/shard_map/ppermute | solution.py:13
  23.2 0.6 multiply_reduce_fusion.4
  24.5 0.6 dynamic-slice
  25.1 0.7 convert_dynamic-update-slice_fusion
  25.8 0.6 dynamic-slice.1
  26.5 16.3 %all-reduce = f32[8]{0:T(128)S(1)} all-reduce(f32[8]{0:T(128)S(1)} %convert_dynamic-update-slice_fusion), channel_id=1, replica_groups=mesh['section'=4,'dp'=8] {'dp'}, use_global_device_ids=true, to_apply=%add | all-reduce | flops 8 | bytes 64
  42.8 14.1 %all-gather.3 = f32[8,1,1024]{2,1,0:T(1,128)S(1)} all-gather(f32[1,1,1024]{2,1,0:T(1,128)S(1)} %multiply_bitcast_fusion), channel_id=1, replica_groups=mesh['section'=4,'dp'=8] {'dp'}, dimensions={0}, use_global_device_ids=true | all-gather | bytes 36864 | tf_op jit(solution)/shard_map/all_gather | solution.py:114
  56.9 0.6 multiply_reduce_fusion.2
  58.2 0.6 multiply_reduce_fusion.1
  59.5 11.8 %psum.7 = bf16[1,1792]{1,0:T(2,128)(2,1)S(1)} all-reduce(bf16[1,1792]{1,0:T(2,128)(2,1)S(1)} %select_n.52), channel_id=1, replica_groups=mesh['section'=4,'dp'=8] {'section'}, use_global_device_ids=true, to_apply=%region_5.0 | all-reduce | flops 1792 | bytes 7168 | tf_op jit(solution)/shard_map/psum | solution.py:18
  71.3 0.3 fusion.50
  71.6 7.2 %all-gather = f32[4096]{0:T(1024)S(1)} all-gather(f32[1024]{0:T(1024)S(1)} %bitcast.99), channel_id=2, replica_groups=mesh['section'=4,'dp'=8] {'section'}, dimensions={0}, use_global_device_ids=true | all-gather | bytes 20480 | tf_op jit(solution)/shard_map/all_gather | solution.py:104
  78.8 0.6 multiply_reduce_fusion.5
  80.1 14.1 %all-gather.1 = f32[8192]{0:T(1024)S(1)} all-gather(f32[1024]{0:T(1024)S(1)} %broadcast_multiply_fusion), channel_id=3, replica_groups=mesh['section'=4,'dp'=8] {'dp'}, dimensions={0}, use_global_device_ids=true | all-gather | bytes 36864 | tf_op jit(solution)/shard_map/all_gather | solution.py:113
  94.2 0.3 fusion.59
  94.5 0.2 fusion.47
  95.0 0.6 subtract_reduce_fusion
  97.1 0.6 multiply_reduce_fusion.3
  97.7 0.7 multiply_convert_fusion.2
  99.0 0.4 fusion.60
  99.6 9.1 %all-reduce.1 = f32[1792]{0:T(1024)S(1)} all-reduce(f32[1792]{0:T(1024)S(1)} %dynamic-update-slice.1), channel_id=4, replica_groups=mesh['section'=4,'dp'=8] {'section'}, use_global_device_ids=true, to_apply=%add.1 | all-reduce | flops 1792 | bytes 14336
  108.7 0.7 fusion.58
  110.6 2.2 %broadcast_select_fusion = bf16[1,1,257,1792]{3,2,1,0:T(8,128)(2,1)} fusion(bf16[1,1,257,1792]{3,2,1,0:T(8,128)(2,1)} %collective-permute-done.1, pred[]{:T(512)S(6)} %eq.8, bf16[1792]{0:T(1024)(128)(2,1)S(1)} %multiply_convert_fusion), kind=kLoop, calls=%fused_computation.40 | loop fusion | flops 460544 | bytes 1845761 | tf_op jit(solution)/shard_map/jit(_where)/select_n | solution.py:138
  112.8 0.9 copy.27
  (44 shorter events, 0.9 us)
Async XLA Ops:
  0.6 70.7 %copy-start = (bf16[448,1024]{1,0:T(8,128)(2,1)S(1)}, bf16[448,1024]{1,0:T(8,128)(2,1)}, u32[]{:S(2)}) copy-start(bf16[448,1024]{1,0:T(8,128)(2,1)} %param.15) | copy-start | bytes 2752516
  0.6 3.2 %copy-start.2 = (bf16[1,1,257,1792]{3,2,1,0:T(8,128)(2,1)S(1)}, bf16[1,1,257,1792]{3,2,1,0:T(8,128)(2,1)}, u32[]{:S(2)}) copy-start(bf16[1,1,257,1792]{3,2,1,0:T(8,128)(2,1)} %param.9) | copy-start | bytes 2763268
  0.7 3.2 %copy-start.6 = (f32[1,1792]{1,0:T(1,128)S(1)}, f32[1,1792]{1,0:T(1,128)}, u32[]{:S(2)}) copy-start(f32[1,1792]{1,0:T(1,128)} %param.13) | copy-start | bytes 21508
  3.9 10.9 %copy-start.1 = (bf16[1,1,257,1792]{3,2,1,0:T(8,128)(2,1)S(1)}, bf16[1,1,257,1792]{3,2,1,0:T(8,128)(2,1)}, u32[]{:S(2)}) copy-start(bf16[1,1,257,1792]{3,2,1,0:T(8,128)(2,1)} %param.10) | copy-start | bytes 2763268
  9.7 5.7 %copy-start.3 = (bf16[1,1,257,1792]{3,2,1,0:T(8,128)(2,1)S(1)}, bf16[1,1,257,1792]{3,2,1,0:T(8,128)(2,1)}, u32[]{:S(2)}) copy-start(bf16[1,1,257,1792]{3,2,1,0:T(8,128)(2,1)} %param.11) | copy-start | bytes 2763268
  9.7 100.9 %collective-permute-start = (bf16[1,1,257,1792]{3,2,1,0:T(8,128)(2,1)}, bf16[1,1,257,1792]{3,2,1,0:T(8,128)(2,1)S(1)}, u32[]{:S(2)}, u32[]{:S(2)}) collective-permute-start(bf16[1,1,257,1792]{3,2,1,0:T(8,128)(2,1)} %bitcast.4), channel_id=1, source_target_pairs={{0,8},{8,16},{16,24},{1,9},{9,17},{17,25},{2,10},{10,18},{18,26},{... | collective-permute-start | bytes 2763272 | tf_op jit(solution)/shard_map/ppermute | solution.py:13
  20.4 2.8 %copy-start.5 = (bf16[1,1024]{1,0:T(2,128)(2,1)S(1)}, bf16[1,1024]{1,0:T(2,128)(2,1)}, u32[]{:S(2)}) copy-start(bf16[1,1024]{1,0:T(2,128)(2,1)} %param.16) | copy-start | bytes 6148
  20.4 4.1 %copy-start.8 = (u32[32]{0:T(128)S(1)}, u32[32]{0:T(128)}, u32[]{:S(2)}) copy-start(u32[32]{0:T(128)} %constant.76) | copy-start | bytes 388
  20.4 5.4 %copy-start.7 = (u32[32]{0:T(128)S(1)}, u32[32]{0:T(128)}, u32[]{:S(2)}) copy-start(u32[32]{0:T(128)} %constant.81) | copy-start | bytes 388
  20.4 39.0 %copy-start.4 = (f32[1792]{0:T(1024)S(1)}, f32[1792]{0:T(1024)}, u32[]{:S(2)}) copy-start(f32[1792]{0:T(1024)} %param.14) | copy-start | bytes 21508
  21.2 89.4 %collective-permute-start.1 = (bf16[1,1,257,1792]{3,2,1,0:T(8,128)(2,1)S(1)}, bf16[1,1,257,1792]{3,2,1,0:T(8,128)(2,1)}, u32[]{:S(2)}, u32[]{:S(2)}) collective-permute-start(bf16[1,1,257,1792]{3,2,1,0:T(8,128)(2,1)S(1)} %fusion.33), channel_id=1, source_target_pairs={{8,0},{16,8},{24,16},{9,1},{17,9},{25,17},{10,2},{18,10},{26,18},{... | collective-permute-start | bytes 2763272 | tf_op jit(solution)/shard_map/ppermute | solution.py:13
